TPU v7x, 32 devices: a whole 2x2x4 slice. The times are simulated.
32 devices in a mesh: dp: 4 (over z), cp: 8 (over y, x, core).
Axes of the slice: x: 2, y: 2, z: 4, core: 2. Of those that a mesh axis runs over, the one named last changes fastest.
Arguments:
- x: bfloat16 [4096, 6144], P(('dp', 'cp')), parts along dimension 0
- k_cache: bfloat16 [65536, 8, 128], P(('dp', 'cp')), parts along dimension 0
- v_cache: bfloat16 [65536, 8, 128], P(('dp', 'cp')), parts along dimension 0
- ln_gain: bfloat16 [6144], replicated
- w_q: bfloat16 [6144, 12288], replicated
- w_k: bfloat16 [6144, 1024], replicated
- w_v: bfloat16 [6144, 1024], replicated
- w_o: bfloat16 [12288, 6144], replicated
- q_gain: bfloat16 [128], replicated
- k_gain: bfloat16 [128], replicated
Outputs:
- output 1: bfloat16 [4096, 6144], P(('dp', 'cp')), parts along dimension 0
- output 2: bfloat16 [4096, 8, 128], P(('dp', 'cp')), parts along dimension 0
- output 3: bfloat16 [4096, 8, 128], P(('dp', 'cp')), parts along dimension 0
There are 4 independent parts. A program takes and returns all parts, laid end to end along the dimension named above; an argument that names none is the same for every part.
All inputs are finite; a program needn't handle non-finite values.
Results may differ from a plain program's by a relative error of at most 0.0105903.
Values are sent between devices in bfloat16 or wider.
A program may use at most 1.5 GiB of HBM per device.

v0:
```python
import functools
import math

import jax
import jax.numpy as jnp
from jax import lax
from jax.experimental import pallas as pl
from jax.experimental.pallas import tpu as pltpu
from jax.sharding import PartitionSpec as P

HEAD_DIM = 128
ROPE_THETA = 1.0e6
NORM_EPS = 1.0e-6
MESH = pl.DeviceIdType.MESH
F32 = jnp.float32
BF16 = jnp.bfloat16

ORD = (0, 1, 2, 4, 3, 5, 6, 7)
SUB = 256
TILE = 512
HEADS = TILE // HEAD_DIM
WBUFS = 3
RAWS = 3
CHIPS = 4


def div(a, b):
    return a // b if isinstance(a, int) else lax.div(a, jnp.int32(b))


def rem(a, b):
    return a % b if isinstance(a, int) else lax.rem(a, jnp.int32(b))


def flip(me, rel):
    out = 0
    for bit in (1, 2, 4):
        mine = rem(div(me, bit), 2)
        out = out + bit * ((1 - mine) if rel & bit else mine)
    return out


def flip_chip(chip, rel):
    return rem(rem(chip, 2) + rem(rel, 2), 2) + 2 * rem(div(chip, 2) + div(rel, 2), 2)


def block_kernel(rows, seg, width,
                 x_in, k_in, v_in, ln_in, kg_in, qg_in, cos_in, sin_in, wq_in, wk_in, wv_in, wo_in,
                 out, k_out, v_out, kt, vt,
                 xres, gains, hbuf, wbuf, raw, stage, vstage, qbuf, kbuf, vbuf, scores, acc, kraw, vraw, kturn, vturn, peak_ref, sum_ref, fade_ref, chunk_max, ahead_ref, outst,
                 wsem, xsem, qsend, qrecv, kvsend, kvrecv, nsend, nrecv, osend, orecv, ksend, krecv, psend, precv, outsem, turnsem,
                 free_sem):
    dp = lax.axis_index("dp")
    me = lax.axis_index("cp")
    chip, core = div(me, 2), rem(me, 2)
    hid = wbuf.shape[1]
    pair = 2 * rows
    new = 8 * rows
    parts = width // TILE
    per_chip = 2 * parts
    tiles = 4 * per_chip
    keys_a = 2 * seg
    keys_b = 2 * seg + new
    coef = math.log2(math.e) * HEAD_DIM ** -0.5
    neg = float("-inf")
    q_tiles = 4 * parts
    p1_tiles = q_tiles + 2
    out_tiles = hid // TILE
    cached = 8 * seg
    others = range(1, CHIPS)
    chunk = hid // 4
    turns = 8
    cleared = acc.shape[0] // (p1_tiles - turns)
    depth = seg // turns

    def device(index):
        return (dp, index)

    partner = flip(me, 1)

    my_rows = pl.ds(pl.multiple_of(core * rows, rows), rows)
    other_rows = pl.ds(pl.multiple_of((1 - core) * rows, rows), rows)
    x_local = pltpu.make_async_copy(x_in, hbuf.at[my_rows, :], xsem.at[0])
    x_local.start()

    barrier = pltpu.get_barrier_semaphore()
    for rel in range(1, 8):
        pl.semaphore_signal(barrier, inc=1, device_id=device(flip(me, rel)), device_id_type=MESH)

    def remote(src, dst, send, recv, index):
        return pltpu.make_async_remote_copy(
            src_ref=src, dst_ref=dst, send_sem=send, recv_sem=recv, device_id=device(index), device_id_type=MESH)

    def tile_of(ref, slot, a):
        return ref.at[slot, pl.ds(a * chunk, chunk), :]

    def fetch_kv(ref, n):
        slot = rem(n, WBUFS)
        for a in range(CHIPS):
            first = pl.multiple_of((2 * a + core) * HEAD_DIM, HEAD_DIM)
            pltpu.make_async_copy(ref.at[:, pl.ds(first, HEAD_DIM)],
                                  wbuf.at[slot, :, pl.ds(a * HEAD_DIM, HEAD_DIM)], wsem.at[slot, a]).start()

    def fetch_q(n):
        slot = rem(n, WBUFS)
        g, part = div(n - 1, parts), rem(n - 1, parts)
        head = 2 * flip_chip(chip, rem(g + 1, 4)) + core
        first = pl.multiple_of(head * width + part * TILE, TILE)
        for a in range(CHIPS):
            pltpu.make_async_copy(wq_in.at[pl.ds(a * chunk, chunk), pl.ds(first, TILE)],
                                  tile_of(wbuf, slot, a), wsem.at[slot, a]).start()

    def fetch_o(m):
        slot = rem(p1_tiles + m, WBUFS)
        first = pl.multiple_of(m * TILE, TILE)
        for a in range(CHIPS):
            top = pl.multiple_of((2 * a + core) * width, width)
            pltpu.make_async_copy(wo_in.at[pl.ds(top, width), pl.ds(first, TILE)],
                                  tile_of(wbuf, slot, a), wsem.at[slot, a]).start()

    def wait_tile(n):
        slot = rem(n, WBUFS)
        for a in range(CHIPS):
            pltpu.make_async_copy(tile_of(wbuf, slot, a), tile_of(wbuf, slot, a), wsem.at[slot, a]).wait()

    def turn_in(c):
        where = pl.ds(pl.multiple_of(c * depth, depth), depth)
        slot = rem(c, RAWS)
        return (pltpu.make_async_copy(k_in.at[where], kraw.at[slot], turnsem.at[0, slot]),
                pltpu.make_async_copy(v_in.at[where], vraw.at[slot], turnsem.at[1, slot]))

    def turn_out(c):
        where = pl.ds(pl.multiple_of(c * depth, depth), depth)
        slot = rem(c, 2)
        return (pltpu.make_async_copy(kturn.at[slot], kt.at[:, where, :], turnsem.at[2, slot]),
                pltpu.make_async_copy(vturn.at[slot], vt.at[:, :, where], turnsem.at[3, slot]))

    def turn(c):
        slot, here = rem(c, 2), rem(c, RAWS)
        acc[pl.ds(0, 8 * depth), :] = kraw[here].astype(F32).reshape(8 * depth, HEAD_DIM)
        acc[pl.ds(8 * depth, 8 * depth), :] = vraw[here].astype(F32).reshape(8 * depth, HEAD_DIM)
        for h in range(8):
            kturn[slot, h] = acc[pl.ds(h, depth, stride=8), :].astype(BF16)
            vturn[slot, h] = acc[pl.ds(8 * depth + h, depth, stride=8), :].T.astype(BF16)

    x_remote = remote(x_in, hbuf.at[my_rows, :], xsem.at[1], xsem.at[2], partner)
    x_local.wait()
    for c in turn_in(0):
        c.start()
    fetch_kv(wk_in, 0)
    for piece in range(1, RAWS):
        for c in turn_in(piece):
            c.start()
    pl.semaphore_wait(barrier, 7)
    x_remote.start()
    fetch_q(1)
    fetch_q(2)

    def kv_copy(p, kind):
        peer = flip(me, ORD[p])
        if kind == 0:
            src, dst = kt.at[peer], kbuf.at[pl.ds(p * seg, seg), :]
        else:
            src, dst = vt.at[peer], vbuf.at[:, pl.ds(p * seg, seg)]
        if p == 0:
            return pltpu.make_async_copy(src, dst, kvrecv.at[kind, 0])
        return remote(src, dst, kvsend.at[kind, p], kvrecv.at[kind, p], peer)

    def kv_send(pair_index):
        for p in (2 * pair_index, 2 * pair_index + 1):
            for kind in range(2):
                kv_copy(p, kind).start()

    def kv_wait(p):
        for kind in range(2):
            if p == 0:
                kv_copy(p, kind).wait()
            else:
                kv_copy(p, kind).wait_recv()

    def normalise(first_row):
        def some(i, carry):
            at = pl.multiple_of(first_row + i * 32, 32)
            wide = hbuf[pl.ds(at, 32), :].astype(F32)
            mean_sq = jnp.sum(wide * wide, axis=-1, keepdims=True) * (1.0 / hid)
            hbuf[pl.ds(at, 32), :] = (wide * lax.rsqrt(mean_sq + NORM_EPS) * gains[:, :hid]).astype(BF16)
            return carry
        lax.fori_loop(0, rows // 32, some, 0)

    for r in range(hid // HEAD_DIM):
        gains[:, r * HEAD_DIM:(r + 1) * HEAD_DIM] = ln_in[r:r + 1, :].astype(F32)
    gains[:, hid:hid + HEAD_DIM] = kg_in[...].astype(F32)
    gains[:, hid + HEAD_DIM:] = qg_in[...].astype(F32)
    normalise(core * rows)
    for c in turn_in(0):
        c.wait()
    turn(0)
    for c in (*turn_out(0), *turn_in(RAWS)):
        c.start()
    x_remote.wait_recv()
    normalise((1 - core) * rows)

    def multiply(n):
        slot = rem(n, WBUFS)
        return jnp.dot(hbuf[...], wbuf[slot], preferred_element_type=F32)

    def rotate(e):
        group, part = div(e + parts - 1, parts), rem(e + parts - 1, parts)
        gain = gains[:, pl.ds(pl.multiple_of(hid + jnp.minimum(e, 1) * HEAD_DIM, HEAD_DIM), HEAD_DIM)]
        cos_tab, sin_tab = cos_in[...], sin_in[...]
        done = []
        for h in range(HEADS):
            vals = raw[:, h * HEAD_DIM:(h + 1) * HEAD_DIM].astype(F32)
            mean_sq = jnp.sum(vals * vals, axis=-1, keepdims=True) * (1.0 / HEAD_DIM)
            vals = vals * lax.rsqrt(mean_sq + NORM_EPS) * gain
            done.append((vals * cos_tab + pltpu.roll(vals, HEAD_DIM // 2, 1) * sin_tab).astype(BF16))
        done = jnp.concatenate(done, axis=1)
        where = pl.ds(pl.multiple_of(part * TILE, TILE), TILE)
        stage[group, :, where] = done
        qbuf[0, :, where] = done

    def q_copy(rel, part):
        cols = pl.ds(pl.multiple_of(part * TILE, TILE), TILE)
        return remote(stage.at[rel, :, cols], qbuf.at[rel, :, cols], qsend.at[rel, part], qrecv.at[rel, part],
                      2 * flip_chip(chip, rel) + core)

    def new_copy(rel, kind):
        other = flip_chip(chip, rel)
        here = pl.ds(pl.multiple_of(cached + chip * pair, pair), pair)
        if kind == 0:
            first = pl.multiple_of((parts - 1) * TILE + other * HEAD_DIM, HEAD_DIM)
            src, dst = stage.at[0, :, pl.ds(first, HEAD_DIM)], kbuf.at[here, :]
        else:
            src, dst = vstage.at[other], vbuf.at[:, here]
        return remote(src, dst, nsend.at[kind, rel], nrecv.at[kind, rel], 2 * other + core)

    def new_heads(kind, a):
        if kind == 0:
            return stage.at[0, :, pl.ds((parts - 1) * TILE + a * HEAD_DIM, HEAD_DIM)]
        return raw.at[:, pl.ds(a * HEAD_DIM, HEAD_DIM)]

    def to_partner(kind, a, parity):
        dst = kturn.at[kind, 2 * a + parity, pl.ds(0, rows), :]
        return remote(new_heads(kind, a).at[other_rows, :], dst, ksend.at[kind, a], krecv.at[kind, a], partner)

    wait_tile(0)
    raw[...] = multiply(0).astype(BF16)
    fetch_q(3)

    def project(turning, n, carry):
        @pl.when(n == 2)
        def _():
            for rel in others:
                new_copy(rel, 0).start()

        @pl.when((n >= 3) & (n < 3 + 3 * parts))
        def _():
            e = n - 2
            q_copy(div(e + parts - 1, parts), rem(e + parts - 1, parts)).start()

        if turning:
            for c in turn_in(n):
                c.wait()

            @pl.when(n >= 2)
            def _():
                for c in turn_out(n - 2):
                    c.wait()
        else:
            @pl.when(n == turns)
            def _():
                for c in (*turn_out(turns - 2), *turn_out(turns - 1)):
                    c.wait()
                for p in range(2):
                    for kind in range(2):
                        kv_copy(p, kind).start()

            @pl.when(n == 3 + 3 * parts)
            def _():
                kv_send(1)

        wait_tile(n)
        rotate(n - 1)
        if turning:
            turn(n)
        else:
            acc[pl.ds(pl.multiple_of((n - turns) * cleared, cleared), cleared), :] = jnp.zeros((cleared, rows), F32)
        raw[...] = multiply(n).astype(BF16)
        if turning:
            for c in turn_out(n):
                c.start()

            @pl.when(n + RAWS < turns)
            def _():
                for c in turn_in(n + RAWS):
                    c.start()

        @pl.when(n + WBUFS <= q_tiles)
        def _():
            fetch_q(n + WBUFS)

        @pl.when(n + WBUFS == q_tiles + 1)
        def _():
            fetch_kv(wv_in, q_tiles + 1)

        @pl.when((n + WBUFS >= p1_tiles) & (n + WBUFS < p1_tiles + WBUFS - 1))
        def _():
            fetch_o(n + WBUFS - p1_tiles)

        return carry

    lax.fori_loop(1, turns, functools.partial(project, True), 0)
    lax.fori_loop(turns, p1_tiles, functools.partial(project, False), 0)

    here = pl.ds(pl.multiple_of(cached + chip * pair, pair), pair)
    for a in range(CHIPS):
        vstage[a] = raw[:, a * HEAD_DIM:(a + 1) * HEAD_DIM].astype(F32).T.astype(BF16)
    kbuf[here, :] = stage[0, :, pl.ds(pl.multiple_of((parts - 1) * TILE + chip * HEAD_DIM, HEAD_DIM), HEAD_DIM)]
    vbuf[:, here] = vstage[chip]

    def acc_rows(t, h):
        return pl.ds(pl.multiple_of((t * HEADS + h) * HEAD_DIM, HEAD_DIM), HEAD_DIM)

    def init(t, carry):
        peak_ref[t] = jnp.full((1, TILE), neg, F32)
        sum_ref[t] = jnp.zeros((1, TILE), F32)
        return carry

    lax.fori_loop(0, tiles, init, 0)
    ahead_ref[...] = (lax.broadcasted_iota(jnp.int32, (SUB, rows), 0)
                      - lax.broadcasted_iota(jnp.int32, (SUB, rows), 1))
    for rel in others:
        new_copy(rel, 1).start()

    def q_tile(rel, half, part):
        some_rows = pl.ds(pl.multiple_of(half * rows, rows), rows)
        block = qbuf[rel, some_rows, pl.ds(pl.multiple_of(part * TILE, TILE), TILE)]
        return jnp.concatenate([block[:, h * HEAD_DIM:(h + 1) * HEAD_DIM] for h in range(HEADS)], axis=0)

    probs = wbuf.at[(p1_tiles + WBUFS - 1) % WBUFS]

    def step(pv=None, sm=None, qk=None, end=None):
        if end is not None:
            finish(*end)
        if pv is not None:
            t_pv, base_pv, keys_pv = pv
            fade_pv = fade_ref[...]
        if sm is not None:
            t_sm, keys_sm = sm
            old = peak_ref[t_sm]
            top = jnp.maximum(old, jnp.max(chunk_max[...], axis=0, keepdims=True) * coef)
            fade = jnp.exp2(old - top)
            peak_ref[t_sm] = top
        if qk is not None:
            rel_qk, half_qk, part_qk, base_qk, keys_qk, has_new = qk
            q = q_tile(rel_qk, half_qk, part_qk)
            first_row = flip_chip(chip, rel_qk) * pair + half_qk * rows if has_new else None
        total = None
        values = None
        peaks = None
        most = max(pv[2] if pv else 0, sm[1] if sm else 0, qk[4] if qk else 0)
        for s in range(most // SUB):
            lines = slice(s * SUB, (s + 1) * SUB)
            if pv is not None and s * SUB < keys_pv:
                v_part = vbuf[:, pl.ds(pl.multiple_of(base_pv + s * SUB, SUB), SUB)]
                o_part = jnp.dot(v_part, probs[lines, :], preferred_element_type=F32)
                values = o_part if values is None else values + o_part
            if sm is not None and s * SUB < keys_sm:
                w = jnp.exp2(scores[lines, :] * coef - top)
                part = jnp.sum(w.reshape(SUB // 8, 8, TILE), axis=0)
                total = part if total is None else total + part
                probs[lines, :] = w.astype(BF16)
            if qk is not None and s * SUB < keys_qk:
                k_part = kbuf[pl.ds(pl.multiple_of(base_qk + s * SUB, SUB), SUB), :]
                sc = lax.dot_general(k_part, q, (((1,), (1,)), ((), ())), preferred_element_type=F32)
                if has_new and s * SUB >= keys_a:
                    seen = ahead_ref[...] <= first_row - (s * SUB - keys_a)
                    sc = jnp.concatenate(
                        [jnp.where(seen, sc[:, h * rows:(h + 1) * rows], neg) for h in range(HEADS)], axis=1)
                scores[lines, :] = sc
                part = jnp.max(sc.reshape(SUB // 8, 8, TILE), axis=0)
                peaks = part if peaks is None else jnp.maximum(peaks, part)
        if qk is not None:
            chunk_max[...] = peaks
        if sm is not None:
            sum_ref[t_sm] = sum_ref[t_sm] * fade + jnp.sum(total, axis=0, keepdims=True)
            fade_ref[...] = fade
        if pv is not None:
            for h in range(HEADS):
                cols = slice(h * rows, (h + 1) * rows)
                acc[acc_rows(t_pv, h), :] = acc[acc_rows(t_pv, h), :] * fade_pv[:, cols] + values[:, cols]

    def finish(rel, half, part):
        t = rel * per_chip + 2 * part + half
        some_rows = pl.ds(pl.multiple_of(half * rows, rows), rows)
        sums = sum_ref[t]
        done = jnp.concatenate(
            [(acc[acc_rows(t, h), :] / sums[:, h * rows:(h + 1) * rows]).T.astype(BF16) for h in range(HEADS)], axis=1)
        stage[rel, some_rows, pl.ds(pl.multiple_of(part * TILE, TILE), TILE)] = done
        hbuf[some_rows, pl.ds(pl.multiple_of(chip * width + part * TILE, TILE), TILE)] = done

    kv_wait(0)
    kv_wait(1)
    for kind in range(2):
        for a in range(CHIPS):
            kturn[kind, 2 * a + core, :rows] = new_heads(kind, a)[my_rows, :]
            to_partner(kind, a, core).start()

    def halves(u):
        part = div(u, 2)
        return u - 2 * part, part

    step(qk=(0, 0, 0, 0, keys_a, False))
    step(sm=(0, keys_a), qk=(0, *halves(1), 0, keys_a, False))

    def below(u, limit):
        return jnp.minimum(jnp.maximum(limit - u, 0), 1)

    def group_a(g, carry):
        visit = div(g, CHIPS)
        rel = g - CHIPS * visit
        for r in others:
            @pl.when(g == r)
            def _():
                for part in range(parts):
                    q_copy(r, part).wait_recv()

        for v in (1, 2):
            @pl.when(g == CHIPS * v)
            def _():
                kv_wait(2 * v)
                kv_wait(2 * v + 1)

        @pl.when(g == 3)
        def _():
            kv_send(2)

        @pl.when(g == 6)
        def _():
            kv_send(3)

        def body_a(u, carry):
            t = rel * per_chip + u
            wrap = below(t, 2)
            step(pv=(t - 2 + tiles * wrap, (visit - wrap) * keys_a, keys_a),
                 sm=(t - 1 + tiles * below(t, 1), keys_a),
                 qk=(rel, *halves(u), visit * keys_a, keys_a, False))
            return carry

        lax.fori_loop(2 * below(g, 1), per_chip, body_a, carry)
        return carry

    lax.fori_loop(0, 3 * CHIPS, group_a, 0)

    kv_wait(6)
    kv_wait(7)
    for rel in others:
        new_copy(rel, 0).wait_recv()
        new_copy(rel, 1).wait_recv()
        new_copy(rel, 0).wait_send()
        for part in range(parts):
            q_copy(rel, part).wait_send()
    for a in range(CHIPS):
        to_partner(0, a, core).wait_send()

    def o_copy(rel, part):
        cols = pl.ds(pl.multiple_of(part * TILE, TILE), TILE)
        there = pl.ds(pl.multiple_of(chip * width + part * TILE, TILE), TILE)
        return remote(stage.at[rel, :, cols], hbuf.at[:, there], osend.at[rel, part], orecv.at[rel, part],
                      2 * flip_chip(chip, rel) + core)

    def o_arrival(rel, part):
        there = pl.ds(pl.multiple_of(flip_chip(chip, rel) * width + part * TILE, TILE), TILE)
        return remote(hbuf.at[:, there], hbuf.at[:, there], osend.at[rel, part], orecv.at[rel, part],
                      2 * flip_chip(chip, rel) + core)

    base_b = 3 * keys_a
    wide = (base_b, keys_b)

    step(pv=(tiles - 2, 2 * keys_a, keys_a), sm=(tiles - 1, keys_a), qk=(3, 0, 0, *wide, True))
    step(pv=(tiles - 1, 2 * keys_a, keys_a), sm=(3 * per_chip, keys_b), qk=(3, *halves(1), *wide, True))
    step(pv=(3 * per_chip, *wide), sm=(3 * per_chip + 1, keys_b), qk=(3, *halves(2), *wide, True))

    def group_b(g, carry):
        rel = 3 - g

        def body_b(u, carry):
            n = g * per_chip + u

            @pl.when((rem(n, 2) == 1) & (n >= 5) & (n < 5 + 3 * per_chip))
            def _():
                done = n - 5
                o_copy(3 - div(done, per_chip), div(rem(done, per_chip), 2)).start()

            t = rel * per_chip + u
            early = below(u, 3)
            step(pv=(t - 2 + 2 * per_chip * below(u, 2), *wide),
                 sm=(t - 1 + 2 * per_chip * below(u, 1), keys_b),
                 qk=(rel, *halves(u), *wide, True),
                 end=(rel + early, *halves(u - 3 + per_chip * early)))
            return carry

        lax.fori_loop(3 * below(g, 1), per_chip, body_b, carry)
        return carry

    lax.fori_loop(0, CHIPS, group_b, 0)
    last = per_chip - 1
    step(pv=(last - 1, *wide), sm=(last, keys_b), end=(0, *halves(last - 2)))
    step(pv=(last, *wide), end=(0, *halves(last - 1)))
    finish(0, *halves(last))
    fetch_o(WBUFS - 1)

    pl.semaphore_signal(free_sem, inc=1, device_id=device(partner), device_id_type=MESH)
    for rel in others:
        for part in range(parts):
            o_arrival(rel, part).wait_recv()
    pl.semaphore_wait(free_sem, 1)

    for kind in range(2):
        for a in range(CHIPS):
            to_partner(kind, a, 1 - core).wait_recv()
        for h in range(8):
            acc[pl.ds(kind * 8 * rows + h, rows, stride=8), :] = kturn[kind, h, :rows].astype(F32)
        flat = acc[pl.ds(kind * 8 * rows, 8 * rows), :].astype(BF16)
        (kraw, vraw)[kind][0, :rows] = flat.reshape(rows, 8, HEAD_DIM)
    new_out = (pltpu.make_async_copy(kraw.at[0, :rows], k_out, turnsem.at[0, 0]),
               pltpu.make_async_copy(vraw.at[0, :rows], v_out, turnsem.at[0, 1]))
    for c in new_out:
        c.start()

    sent, got, own = 0, out_tiles * rows, 2 * out_tiles * rows

    def lines(first, m):
        return pl.ds(pl.multiple_of(first + m * rows, rows), rows)

    def p_copy(m):
        return remote(scores.at[lines(sent, m), :], scores.at[lines(got, m), :], psend.at[m], precv.at[m], partner)

    def out_copy(m):
        cols = pl.ds(pl.multiple_of(m * TILE, TILE), TILE)
        return pltpu.make_async_copy(outst.at[rem(m, 2)], out.at[:, cols], outsem.at[m])

    def x_copy(m):
        cols = pl.ds(pl.multiple_of(m * TILE, TILE), TILE)
        return pltpu.make_async_copy(x_in.at[:, cols], xres.at[rem(m, 2)], xsem.at[3 + rem(m, 2)])

    def combine(m):
        if isinstance(m, int):
            out_copy(m - 2).wait()
        else:
            @pl.when(m >= 2)
            def _():
                out_copy(m - 2).wait()
        p_copy(m).wait_recv()
        x_copy(m).wait()
        both = scores[lines(own, m), :] + scores[lines(got, m), :]
        outst[rem(m, 2)] = (xres[rem(m, 2)].astype(F32) + both).astype(BF16)
        out_copy(m).start()

    def output(m, carry):
        @pl.when(m >= 1)
        def _():
            p_copy(m - 1).start()

        @pl.when(m >= 2)
        def _():
            combine(m - 2)

        x_copy(m).start()
        wait_tile(p1_tiles + m)
        both = multiply(p1_tiles + m)
        scores[lines(own, m), :] = jnp.where(core == 0, both[:rows], both[rows:])
        scores[lines(sent, m), :] = jnp.where(core == 0, both[rows:], both[:rows])

        @pl.when(m + WBUFS < out_tiles)
        def _():
            fetch_o(m + WBUFS)

        return carry

    lax.fori_loop(0, out_tiles, output, 0)
    p_copy(out_tiles - 1).start()
    combine(out_tiles - 2)
    combine(out_tiles - 1)

    def drain(m, carry):
        p_copy(m).wait_send()
        return carry

    lax.fori_loop(0, out_tiles, drain, 0)
    out_copy(out_tiles - 2).wait()
    out_copy(out_tiles - 1).wait()
    x_remote.wait_send()
    for p in range(1, 8):
        for kind in range(2):
            kv_copy(p, kind).wait_send()
    for rel in others:
        new_copy(rel, 1).wait_send()
        for part in range(parts):
            o_copy(rel, part).wait_send()
    for a in range(CHIPS):
        to_partner(1, a, core).wait_send()
    for c in new_out:
        c.wait()


def block(x, k_cache, v_cache, ln_gain, k_gain, q_gain, cos_tab, sin_tab, w_q, w_k, w_v, w_o):
    rows, hid = x.shape
    seg = k_cache.shape[0]
    width = w_q.shape[1] // 8
    pair, new = 2 * rows, 8 * rows
    parts = width // TILE
    tiles = 8 * parts
    out_tiles = hid // TILE
    keys_b = 2 * seg + new
    cached = 8 * seg
    flops = 4 * (cached + new) * 8 * rows * width + 8 * rows * hid * width * 2
    hbm = pl.BlockSpec(memory_space=pl.ANY)
    vmem = pl.BlockSpec(memory_space=pltpu.VMEM)
    dma = pltpu.SemaphoreType.DMA
    return pl.pallas_call(
        functools.partial(block_kernel, rows, seg, width),
        out_shape=(
            jax.ShapeDtypeStruct((rows, hid), BF16),
            jax.ShapeDtypeStruct((rows, 8, HEAD_DIM), BF16),
            jax.ShapeDtypeStruct((rows, 8, HEAD_DIM), BF16),
            jax.ShapeDtypeStruct((8, seg, HEAD_DIM), BF16),
            jax.ShapeDtypeStruct((8, HEAD_DIM, seg), BF16),
        ),
        in_specs=[hbm, hbm, hbm, vmem, vmem, vmem, vmem, vmem, hbm, hbm, hbm, hbm],
        out_specs=(hbm,) * 5,
        scratch_shapes=[
            pltpu.VMEM((2, rows, TILE), BF16),
            pltpu.VMEM((1, hid + 2 * HEAD_DIM), F32),
            pltpu.VMEM((pair, hid), BF16),
            pltpu.VMEM((WBUFS, hid, TILE), BF16),
            pltpu.VMEM((pair, TILE), BF16),
            pltpu.VMEM((5, pair, width), BF16),
            pltpu.VMEM((4, HEAD_DIM, pair), BF16),
            pltpu.VMEM((4, pair, width), BF16),
            pltpu.VMEM((cached + new, HEAD_DIM), BF16),
            pltpu.VMEM((HEAD_DIM, cached + new), BF16),
            pltpu.VMEM((max(keys_b, 3 * out_tiles * rows), TILE), F32),
            pltpu.VMEM((tiles * HEADS * HEAD_DIM, rows), F32),
            pltpu.VMEM((RAWS, seg // 8, 8, HEAD_DIM), BF16),
            pltpu.VMEM((RAWS, seg // 8, 8, HEAD_DIM), BF16),
            pltpu.VMEM((2, 8, seg // 8, HEAD_DIM), BF16),
            pltpu.VMEM((2, 8, HEAD_DIM, seg // 8), BF16),
            pltpu.VMEM((tiles, 1, TILE), F32),
            pltpu.VMEM((tiles, 1, TILE), F32),
            pltpu.VMEM((1, TILE), F32),
            pltpu.VMEM((8, TILE), F32),
            pltpu.VMEM((SUB, rows), jnp.int32),
            pltpu.VMEM((2, rows, TILE), BF16),
            dma((WBUFS, 4)),
            dma((5,)),
            dma((4, parts)), dma((4, parts)),
            dma((2, 8)), dma((2, 8)),
            dma((2, 4)), dma((2, 4)),
            dma((4, parts)), dma((4, parts)),
            dma((2, 4)), dma((2, 4)),
            dma((out_tiles,)), dma((out_tiles,)),
            dma((out_tiles,)),
            dma((4, RAWS)),
            pltpu.SemaphoreType.REGULAR,
        ],
        compiler_params=pltpu.CompilerParams(
            collective_id=0, has_side_effects=True, vmem_limit_bytes=67043328),
        cost_estimate=pl.CostEstimate(flops=flops, bytes_accessed=200 * 1024 * 1024, transcendentals=flops // 512),
        name="block",
    )(x, k_cache, v_cache, ln_gain, k_gain, q_gain, cos_tab, sin_tab, w_q, w_k, w_v, w_o)


def hand_over(*results):
    pieces = 4

    def copy(*refs):
        count = len(results)
        sources, targets, held, sems = refs[:count], refs[count:2 * count], refs[2 * count:3 * count], refs[-1]
        copies = []
        for i, (source, target, middle) in enumerate(zip(sources, targets, held)):
            some = source.shape[0] // pieces
            for j in range(pieces):
                at = pl.ds(j * some, some)
                copies.append((pltpu.make_async_copy(source.at[at], middle.at[at], sems.at[0, i, j]),
                               pltpu.make_async_copy(middle.at[at], target.at[at], sems.at[1, i, j])))
        for into, _ in copies:
            into.start()
        for into, back in copies:
            into.wait()
            back.start()
        for _, back in copies:
            back.wait()

    hbm = pl.BlockSpec(memory_space=pl.ANY)
    return pl.pallas_call(
        copy,
        out_shape=tuple(jax.ShapeDtypeStruct(a.shape, a.dtype) for a in results),
        in_specs=[hbm] * len(results),
        out_specs=(hbm,) * len(results),
        scratch_shapes=[*(pltpu.VMEM(a.shape, a.dtype) for a in results),
                        pltpu.SemaphoreType.DMA((2, len(results), pieces))],
        name="hand_over",
    )(*results)


def solution(mesh):
    cp_size = mesh.shape['cp']
    row_spec = P(('dp', 'cp'), None)
    cache_spec = P(('dp', 'cp'), None, None)
    whole = P()

    def device_step(x_rows, k_cache, v_cache, ln_gain, w_q, w_k, w_v, w_o, q_gain, k_gain):
        rows = x_rows.shape[0]
        prefix_len = k_cache.shape[0] * cp_size
        chip = lax.axis_index('cp') // 2
        positions = (prefix_len + chip * 2 * rows + jnp.arange(2 * rows)).astype(F32)
        lane = jnp.arange(HEAD_DIM)
        half = HEAD_DIM // 2
        inv_freq = ROPE_THETA ** (-(lane % half).astype(F32) * (2.0 / HEAD_DIM))
        angles = positions[:, None] * inv_freq[None, :]
        cos_tab = jnp.cos(angles)
        sin_tab = jnp.sin(angles) * jnp.where(lane < half, -1.0, 1.0)[None, :]
        out, k_new, v_new, _, _ = block(
            x_rows, k_cache, v_cache, ln_gain.reshape(-1, HEAD_DIM), k_gain[None, :], q_gain[None, :], cos_tab, sin_tab, w_q, w_k, w_v, w_o)
        return hand_over(out, k_new, v_new)

    return jax.shard_map(device_step, mesh=mesh, in_specs=(row_spec, cache_spec, cache_spec, whole, whole, whole, whole, whole, whole, whole), out_specs=(row_spec, cache_spec, cache_spec), check_vma=False)
```

profile of v0, /device:TPU:0, one launch (start us, length us, event | category | flops | bytes accessed | tf_op | source)
XLA Modules:
  0.0 265.3 jit_solution(4878866692828357996)
XLA Ops:
  0.7 1.2 fusion
  1.9 260.7 %block.1 = (bf16[128,6144]{1,0:T(8,128)(2,1)}, bf16[128,8,128]{2,1,0:T(8,128)(2,1)}, bf16[128,8,128]{2,1,0:T(8,128)(2,1)}, bf16[8,2048,128]{2,1,0:T(8,128)(2,1)}, bf16[8,128,2048]{2,1,0:T(8,128)(2,1)}) custom-call(bf16[128,6144]{1,0:T(8,128)(2,1)} %x_in.1, bf16[2048,8,128]{2,1,0:T(8,128)(2,1)} %k_in.1, bf16[2048,8,128]{2,1,0:T(8,128)(2,1)} %v_in.1, ...), custom_call_target="tpu_custom_call" | custom-call | flops 128849018880 | bytes 209715200 | tf_op jit(solution)/shard_map/block/pallas_call | solution.py:621
  262.6 2.5 hand_over.1
  (2 shorter events, 0.0 us)
where the time goes:
time: 265 us
  Pallas kernels  263 us (99%)
    pallas_call x1, Pallas kernels, block(): pl.pallas_call(functools.partial(block_kernel, rows, seg, width), out_sha...  261 us

commit v1 on v0

--- a/solution.py
+++ b/solution.py
@@ -355,12 +355,19 @@
             rel_qk, half_qk, part_qk, base_qk, keys_qk, has_new = qk
             q = q_tile(rel_qk, half_qk, part_qk)
             first_row = flip_chip(chip, rel_qk) * pair + half_qk * rows if has_new else None
+
+        def scores_of(s):
+            k_part = kbuf[pl.ds(pl.multiple_of(base_qk + s * SUB, SUB), SUB), :]
+            return lax.dot_general(k_part, q, (((1,), (1,)), ((), ())), preferred_element_type=F32)
+
         total = None
         values = None
         peaks = None
         most = max(pv[2] if pv else 0, sm[1] if sm else 0, qk[4] if qk else 0)
         for s in range(most // SUB):
             lines = slice(s * SUB, (s + 1) * SUB)
+            if qk is not None and s * SUB < keys_qk and has_new:
+                sc = scores_of(s)
             if pv is not None and s * SUB < keys_pv:
                 v_part = vbuf[:, pl.ds(pl.multiple_of(base_pv + s * SUB, SUB), SUB)]
                 o_part = jnp.dot(v_part, probs[lines, :], preferred_element_type=F32)
@@ -371,8 +378,8 @@
                 total = part if total is None else total + part
                 probs[lines, :] = w.astype(BF16)
             if qk is not None and s * SUB < keys_qk:
-                k_part = kbuf[pl.ds(pl.multiple_of(base_qk + s * SUB, SUB), SUB), :]
-                sc = lax.dot_general(k_part, q, (((1,), (1,)), ((), ())), preferred_element_type=F32)
+                if not has_new:
+                    sc = scores_of(s)
                 if has_new and s * SUB >= keys_a:
                     seen = ahead_ref[...] <= first_row - (s * SUB - keys_a)
                     sc = jnp.concatenate(

time: 265 us -> 264 us (level)
  no operation moved by 1% of the time
where the time goes in v1:
time: 264 us
  Pallas kernels  262 us (99%)
    pallas_call x1, Pallas kernels, block(): pl.pallas_call(functools.partial(block_kernel, rows, seg, width), out_sha...  259 us

profile of v1, /device:TPU:0, one launch (start us, length us, event | category | flops | bytes accessed | tf_op | source)
XLA Modules:
  0.0 263.9 jit_solution(12774550969214631107)
XLA Ops:
  0.7 1.2 fusion
  1.9 259.3 %block.1 = (bf16[128,6144]{1,0:T(8,128)(2,1)}, bf16[128,8,128]{2,1,0:T(8,128)(2,1)}, bf16[128,8,128]{2,1,0:T(8,128)(2,1)}, bf16[8,2048,128]{2,1,0:T(8,128)(2,1)}, bf16[8,128,2048]{2,1,0:T(8,128)(2,1)}) custom-call(bf16[128,6144]{1,0:T(8,128)(2,1)} %x_in.1, bf16[2048,8,128]{2,1,0:T(8,128)(2,1)} %k_in.1, bf16[2048,8,128]{2,1,0:T(8,128)(2,1)} %v_in.1, ...), custom_call_target="tpu_custom_call" | custom-call | flops 128849018880 | bytes 209715200 | tf_op jit(solution)/shard_map/block/pallas_call | solution.py:628
  261.2 2.5 hand_over.1
  (2 shorter events, 0.0 us)
